TPU v7x, 32 devices: a whole 2x2x4 slice. The times are simulated.
32 devices in a mesh: mem: 16 (over z, y, x), tile: 2 (over core).
Axes of the slice: x: 2, y: 2, z: 4, core: 2. Of those that a mesh axis runs over, the one named last changes fastest.
Arguments:
- starting_samples: float32 [512, 128, 256], P('mem', 'tile'), may hold values from -6 to 6
- transport_number_vertical: float32 [128, 256], P('tile'), may hold values from 0.1 to 0.35
- transport_number_horizontal: float32 [128, 256], P('tile'), may hold values from 0.1 to 0.35
- spreading_number: float32 [128, 256], P('tile'), may hold values from 0.01 to 0.07
- obs_value: float32 [2, 16, 128], P('tile'), may hold values from -6 to 6
- obs_error: float32 [2, 16, 128], P('tile'), may hold values from 0.002 to 0.05
- obs_index: int32 [2, 16, 128], P('tile'), may hold values from 0 to 1023
- loc_index: int32 [2, 16, 128], P('tile'), may hold values from 0 to 7
- loc_table: float32 [3, 8], replicated, may hold values from 0.2 to 1
Outputs:
- analysis: float32 [512, 128, 256], P('mem', 'tile')
Inputs may be any that keep to these rules, and one draw needn't show every extreme that they name: Observation j of a patch lies in the patch's cell obs_index, cells numbered row by row, 16 to a row.
All inputs are finite; a program needn't handle non-finite values.
Results may differ from a plain program's by a relative error of at most 0.0003.
Values sent between devices are 32-bit elements; how exact they have to be, the bound alone decides.
No kernel may reach another device: no remote copies, remote signals or barrier semaphores. Data moves between devices by JAX's collectives and lax.ppermute only.
A program may use at most 128 MiB of HBM per device.

v0:
```python
import functools

import jax
import jax.numpy as jnp
from jax import lax
from jax.experimental import pallas as pl
from jax.experimental.pallas import tpu as pltpu
from jax.sharding import PartitionSpec as P


PASSES = 6
NS_ITERS = 8
HALO = 8
LINES = 16
F32 = jnp.float32
BF16 = jnp.bfloat16
VMEM = pl.BlockSpec(memory_space=pltpu.VMEM)
SMEM = pl.BlockSpec(memory_space=pltpu.SMEM)


def split(x):
    high = x.astype(BF16)
    return high, (x - high.astype(F32)).astype(BF16)


def dot_split(a, b, dims=(((1,), (0,)), ((), ()))):
    (ah, al), (bh, bl) = a, b
    dot = functools.partial(lax.dot_general, dimension_numbers=dims, preferred_element_type=F32)
    return dot(ah, bh) + (dot(ah, bl) + dot(al, bh))


def swap_granules(rows, lane, width):
    count = len(rows)
    rows = list(rows)
    step = count // 2
    while step:
        odd = (lane // (width * step)) % 2 == 1
        for i in range(count):
            if i & step:
                continue
            a, b = rows[i], rows[i + step]
            rows[i] = jnp.where(odd, pltpu.roll(b, width * step, axis=1), a)
            rows[i + step] = jnp.where(odd, b, pltpu.roll(a, 128 - width * step, axis=1))
        step //= 2
    return rows


def forecast_kernel(blocks, x_ref, up_ref, down_ref, av_ref, ah_ref, sp_ref, index_ref, fields, seen, one, two, coef):
    members, rows, columns = x_ref.shape
    total = rows + 2 * HALO
    width = columns // blocks
    per = 128 // width
    cells = rows * width

    def place(source, member, row, target):
        tile = source[pl.ds(member, 8), pl.ds(row, 8), :]
        one[pl.ds(target, 8), pl.ds(member, 8), :] = jnp.swapaxes(tile, 0, 1)

    def load_rows(t, carry):
        row = pl.multiple_of(t * 8, 8)
        for m in range(0, members, 8):
            place(x_ref, m, row, HALO + row)
        return carry

    lax.fori_loop(0, rows // 8, load_rows, 0)
    for m in range(0, members, 8):
        place(up_ref, m, 0, 0)
        place(down_ref, m, 0, HALO + rows)

    def spread_coef(av, ah, sp, target):
        for n, value in enumerate((1.0 - av - ah - 4.0 * sp, av + sp, ah + sp, sp)):
            for i in range(8):
                coef[n, target + i] = jnp.broadcast_to(value[i : i + 1], (8, columns))

    spread_coef(up_ref[members], up_ref[members + 1], up_ref[members + 2], 0)
    spread_coef(down_ref[members], down_ref[members + 1], down_ref[members + 2], HALO + rows)

    def coef_rows(t, carry):
        row = pl.multiple_of(t * 8, 8)
        spread_coef(av_ref[pl.ds(row, 8), :], ah_ref[pl.ds(row, 8), :], sp_ref[pl.ds(row, 8), :], HALO + row)
        return carry

    lax.fori_loop(0, rows // 8, coef_rows, 0)

    def wide(value):
        return jnp.concatenate([value] * (members // 8), axis=0)

    buffers = (one, two)
    for step in range(1, PASSES + 1):
        source, target = buffers[(step - 1) % 2], buffers[step % 2]
        first = HALO - PASSES + step
        count = total - 2 * first

        def advance(row, lines, source=source, target=target):
            middle = [source[row + i] for i in range(-1, lines + 1)]
            west = [pltpu.roll(m, 1, axis=1) for m in middle[1:-1]]
            east = [pltpu.roll(m, columns - 1, axis=1) for m in middle[1:-1]]
            for i in range(lines):
                target[row + i] = (
                    wide(coef[0, row + i]) * middle[i + 1]
                    + wide(coef[2, row + i]) * middle[i]
                    + wide(coef[1, row + i]) * west[i]
                    + wide(coef[3, row + i]) * (middle[i + 2] + east[i])
                )

        def sweep(t, carry, first=first, advance=advance):
            advance(first + LINES * t, LINES)
            return carry

        lax.fori_loop(0, count // LINES, sweep, 0)
        if count % LINES:
            advance(first + count // LINES * LINES, count % LINES)

    final = buffers[PASSES % 2]
    lane = lax.broadcasted_iota(jnp.int32, (members, 128), 1)

    def cut(t, carry):
        row = HALO + t * per
        at = pl.multiple_of(t * 128, 128)
        for h in range(columns // 128):
            lines = [final[row + i, :, h * 128 : (h + 1) * 128] for i in range(per)]
            for j, piece in enumerate(swap_granules(lines, lane, width)):
                fields[h * per + j, :, pl.ds(at, 128)] = piece
        return carry

    lax.fori_loop(0, rows // per, cut, 0)

    def look(b, carry):
        index = jnp.broadcast_to(index_ref[b], (members, 128))
        low, high = index % 128, index // 128
        value = jnp.zeros((members, 128), F32)
        for t in range(cells // 128):
            part = fields[b, :, t * 128 : (t + 1) * 128]
            picked = jnp.take_along_axis(part, low, axis=1, mode="promise_in_bounds")
            value = jnp.where(high == t, picked, value)
        seen[b] = value
        return carry

    lax.fori_loop(0, blocks, look, 0)


def weight_kernel(partner_ref, own_ref, left_ref, right_ref, prec_ref, value_ref, high_ref, low_ref, stacked, innovation, mh, ml, zh, zl, fh, fl):
    blocks, chunk, nobs = own_ref.shape
    size = blocks * chunk
    for role, ref in enumerate((left_ref, own_ref, right_ref)):
        piece = ref[...].reshape(size, nobs)
        mean = jnp.sum(piece, axis=0, keepdims=True) * (1.0 / size)
        stacked[:, role * nobs : (role + 1) * nobs] = piece - mean
        innovation[:, role * nobs : (role + 1) * nobs] = value_ref[:, role * nobs : (role + 1) * nobs] - mean
    prec = prec_ref[...]
    spread = stacked[...]
    pull = jnp.sum(spread * (prec * innovation[...]), axis=1, keepdims=True)
    contract = (((1,), (1,)), ((), ()))
    gram = dot_split(split(spread * prec), split(spread), contract)
    eye = lax.broadcasted_iota(jnp.int32, (size, size), 0) == lax.broadcasted_iota(jnp.int32, (size, size), 1)
    gram = gram + jnp.where(eye, size - 1.0, 0.0)
    total = jnp.sum(jnp.sum(gram * gram, axis=0, keepdims=True), axis=1, keepdims=True)
    scale = lax.rsqrt(total)
    norm = jnp.sqrt(total)
    matrix = gram / norm

    def factor_of(product):
        diagonal = lax.broadcasted_iota(jnp.int32, (size, size), 0) == lax.broadcasted_iota(jnp.int32, (size, size), 1)
        return jnp.where(diagonal, 1.5, 0.0) - 0.5 * product

    mh[...], ml[...] = split(matrix)
    fh[...], fl[...] = split(factor_of(matrix))
    zh[...], zl[...] = fh[...], fl[...]
    mh[...], ml[...] = split(dot_split((mh[...], ml[...]), (fh[...], fl[...])))

    def iterate(step, carry):
        fh[...], fl[...] = split(factor_of(dot_split((zh[...], zl[...]), (mh[...], ml[...]))))
        mh[...], ml[...] = split(dot_split((mh[...], ml[...]), (fh[...], fl[...])))
        zh[...], zl[...] = split(dot_split((fh[...], fl[...]), (zh[...], zl[...])))
        return carry

    lax.fori_loop(0, NS_ITERS - 2, iterate, 0)
    fh[...], fl[...] = split(factor_of(dot_split((zh[...], zl[...]), (mh[...], ml[...]))))
    root = dot_split((fh[...], fl[...]), (zh[...], zl[...]))
    line = jnp.transpose(jnp.broadcast_to(pull, (size, 128)))[0:1]
    once = jnp.sum(root * line, axis=1, keepdims=True)
    twice = jnp.sum(root * once, axis=0, keepdims=True) / norm
    fh[...], fl[...] = split(jnp.sqrt((size - 1.0) * scale) * root + twice)
    for k in range(blocks):
        row = pl.multiple_of(partner_ref[k] * chunk, chunk)
        high_ref[k * chunk : (k + 1) * chunk, :] = fh[pl.ds(row, chunk), :]
        low_ref[k * chunk : (k + 1) * chunk, :] = fl[pl.ds(row, chunk), :]


def analysis_kernel(high_ref, low_ref, fields, *rest):
    outs, (ah, al, center) = rest[:-3], rest[-3:]
    blocks, chunk, _ = fields.shape
    size = blocks * chunk
    total = fields[0]
    for k in range(1, blocks):
        total = total + fields[k]
    center[...] = jnp.sum(total, axis=0, keepdims=True) * (1.0 / size)
    for k in range(blocks):
        high, low = split(fields[k] - center[...])
        ah[k * chunk : (k + 1) * chunk, :] = high
        al[k * chunk : (k + 1) * chunk, :] = low
    result = dot_split((high_ref[...], low_ref[...]), (ah[...], al[...]))
    for k in range(blocks):
        outs[k][...] = result[k * chunk : (k + 1) * chunk, :] + center[...]


def assemble_kernel(blocks, partner_ref, *rest):
    pieces, (out_ref, fields, lines_ref) = rest[:blocks], rest[blocks:]
    members, rows, columns = out_ref.shape
    for k in range(blocks):
        fields[partner_ref[k]] = pieces[k][...]
    width = columns // blocks
    per = 128 // width
    lane = lax.broadcasted_iota(jnp.int32, (members, 128), 1)

    def join(t, carry):
        at = pl.multiple_of(t * 128, 128)
        for h in range(columns // 128):
            granules = [fields[h * per + j, :, pl.ds(at, 128)] for j in range(per)]
            for i, line in enumerate(swap_granules(granules, lane, width)):
                lines_ref[i, :, h * 128 : (h + 1) * 128] = line
        row = pl.multiple_of(t * per, 8)
        for m in range(0, members, 8):
            tile = lines_ref[:, m : m + 8, :]
            out_ref[m : m + 8, pl.ds(row, 8), :] = jnp.swapaxes(tile, 0, 1)
        return carry

    lax.fori_loop(0, rows // per, join, 0)


def cost(flops, moved):
    return pl.CostEstimate(flops=int(flops), bytes_accessed=int(moved), transcendentals=0)


def shape(dims, dtype=F32):
    return jax.ShapeDtypeStruct(dims, dtype)


PARAMS = pltpu.CompilerParams(vmem_limit_bytes=56 * 1024 * 1024)


def body(
    starting_samples,
    transport_number_vertical,
    transport_number_horizontal,
    spreading_number,
    obs_value,
    obs_error,
    obs_index,
    loc_index,
    loc_table,
):
    blocks = lax.axis_size("mem")
    tiles = lax.axis_size("tile")
    members, rows, columns = starting_samples.shape
    nobs = obs_index.shape[2]
    cells = rows * (columns // blocks)
    size = blocks * members
    me = lax.axis_index("mem")

    coefs = (transport_number_vertical, transport_number_horizontal, spreading_number)

    def edge(part):
        return jnp.concatenate([starting_samples[:, part]] + [c[None, part] for c in coefs], axis=0)

    up = [(i, (i + 1) % tiles) for i in range(tiles)]
    down = [(j, i) for i, j in up]
    above = lax.ppermute(edge(slice(rows - HALO, rows)), "tile", up)
    below = lax.ppermute(edge(slice(0, HALO)), "tile", down)

    fields, seen = pl.pallas_call(
        functools.partial(forecast_kernel, blocks),
        out_shape=[shape((blocks, members, cells)), shape((blocks, members, nobs))],
        in_specs=[VMEM] * 7,
        out_specs=[VMEM] * 2,
        scratch_shapes=[
            pltpu.VMEM((rows + 2 * HALO, members, columns), F32),
            pltpu.VMEM((rows + 2 * HALO, members, columns), F32),
            pltpu.VMEM((4, rows + 2 * HALO, 8, columns), F32),
        ],
        compiler_params=PARAMS,
        cost_estimate=cost(5e6, 5e6),
        name="forecast",
    )(starting_samples, above, below, *coefs, obs_index[0][:, None, :])

    seen, obs_value, obs_error, loc_index = lax.optimization_barrier((seen, obs_value, obs_error, loc_index))
    own = lax.all_to_all(seen, "mem", 0, 0)
    roles = (me + jnp.arange(3, dtype=jnp.int32) - 1) % blocks
    onehot = (loc_index[0][roles][:, :, None] == jnp.arange(loc_table.shape[1], dtype=jnp.int32)).astype(F32)
    precision = jnp.sum(onehot * loc_table[:, None, :], axis=2) / obs_error[0][roles]
    values = obs_value[0][roles]
    partner = jnp.bitwise_xor(me, jnp.arange(blocks, dtype=jnp.int32))
    own, precision, values, partner = lax.optimization_barrier((own, precision, values, partner))
    ring = [(i, (i + 1) % blocks) for i in range(blocks)]
    left = lax.ppermute(own, "mem", ring)
    right = lax.ppermute(own, "mem", [(j, i) for i, j in ring])
    fields = lax.all_to_all(fields, "mem", 0, 0)

    high, low = pl.pallas_call(
        weight_kernel,
        out_shape=[shape((size, size), BF16)] * 2,
        in_specs=[SMEM] + [VMEM] * 5,
        out_specs=[VMEM] * 2,
        scratch_shapes=[pltpu.VMEM((size, 3 * nobs), F32), pltpu.VMEM((1, 3 * nobs), F32)]
        + [pltpu.VMEM((size, size), BF16)] * 6,
        compiler_params=PARAMS,
        cost_estimate=cost(5e9, 5e6),
        name="weight",
    )(partner, own, left, right, precision.reshape(1, -1), values.reshape(1, -1))

    result = pl.pallas_call(
        analysis_kernel,
        out_shape=[shape((members, cells))] * blocks,
        in_specs=[VMEM] * 3,
        out_specs=[VMEM] * blocks,
        scratch_shapes=[pltpu.VMEM((size, cells), BF16)] * 2 + [pltpu.VMEM((1, cells), F32)],
        compiler_params=PARAMS,
        cost_estimate=cost(1e9, 5e6),
        name="analysis",
    )(high, low, fields)

    back = {0: result[0]}
    for k in sorted(range(1, blocks), reverse=True):
        back[k] = lax.ppermute(result[k], "mem", [(i, i ^ k) for i in range(blocks)])
    return pl.pallas_call(
        functools.partial(assemble_kernel, blocks),
        out_shape=shape((members, rows, columns)),
        in_specs=[SMEM] + [VMEM] * blocks,
        out_specs=VMEM,
        scratch_shapes=[pltpu.VMEM((blocks, members, cells), F32), pltpu.VMEM((8, members, columns), F32)],
        compiler_params=PARAMS,
        cost_estimate=cost(1e6, 5e6),
        name="assemble",
    )(partner, *[back[k] for k in range(blocks)])


def solution(mesh):
    in_specs = (
        P("mem", "tile", None),
        P("tile", None),
        P("tile", None),
        P("tile", None),
        P("tile", None, None),
        P("tile", None, None),
        P("tile", None, None),
        P("tile", None, None),
        P(),
    )
    out_specs = P("mem", "tile", None)
    return jax.shard_map(body, mesh=mesh, in_specs=in_specs, out_specs=out_specs, check_vma=False)
```

profile of v0, /device:TPU:12, one launch (start us, length us, event | category | flops | bytes accessed | tf_op | source)
XLA Modules:
  0.0 193.2 jit_solution(5180800390347308221)
XLA Ops:
  5.3 18.9 %forecast.1 = (f32[16,32,1024]{2,1,0:T(8,128)}, f32[16,32,128]{2,1,0:T(8,128)}) custom-call(f32[32,64,256]{2,1,0:T(8,128)} %x_ref.1, f32[35,8,256]{2,1,0:T(8,128)} %copy-done.2, f32[35,8,256]{2,1,0:T(8,128)} %copy-done.3, f32[64,256]{1,0:T(8,128)} %av_ref.1, f32[64,256]{1,0:T(8,128)} %ah_ref.1, f32[64,256]{1,0:T(8,128)} %sp_ref.1, s32[16,1,128]{2,1,0:T(1,128)} %bitcast.31), custom_call_target="tpu_custom_call" | custom-call | flops 5000000 | bytes 5000000 | tf_op jit(solution)/shard_map/forecast/pallas_call | solution.py:271
  24.2 15.8 %all_to_all.10.own_ref = f32[16,32,128]{2,1,0:T(8,128)S(1)} all-to-all(f32[16,32,128]{2,1,0:T(8,128)} %get-tuple-element.34), channel_id=1, replica_groups=mesh['mem'=16,'tile'=2] {'mem'}, dimensions={0} | all-to-all | bytes 524288 | tf_op jit(solution)/shard_map/all_to_all | solution.py:287
  40.0 5.3 %all-to-all-start.1 = ((f32[16,32,1024]{2,1,0:T(8,128)}), f32[16,32,1024]{2,1,0:T(8,128)S(1)}, u32[]{:S(2)}, u32[]{:S(2)}) async-start(f32[16,32,1024]{2,1,0:T(8,128)} %get-tuple-element.44), calls=%async_computation.1 | async-start | bytes 4194304 | tf_op jit(solution)/shard_map/all_to_all | solution.py:297
  51.0 14.1 %collective-permute-done.3.right_ref = f32[16,32,128]{2,1,0:T(8,128)S(1)} collective-permute-done((f32[16,32,128]{2,1,0:T(8,128)S(1)}, f32[16,32,128]{2,1,0:T(8,128)S(1)}, u32[]{:S(2)}, u32[]{:S(2)}) %collective-permute-start.3) | collective-permute-done | bytes 262176 | tf_op jit(solution)/shard_map/ppermute | solution.py:296
  65.1 10.2 %collective-permute-done.2.left_ref = f32[16,32,128]{2,1,0:T(8,128)S(1)} collective-permute-done((f32[16,32,128]{2,1,0:T(8,128)S(1)}, f32[16,32,128]{2,1,0:T(8,128)S(1)}, u32[]{:S(2)}, u32[]{:S(2)}) %collective-permute-start.2) | collective-permute-done | bytes 262176 | tf_op jit(solution)/shard_map/ppermute | solution.py:295
  76.1 23.7 %weight.1 = (bf16[512,512]{1,0:T(8,128)(2,1)}, bf16[512,512]{1,0:T(8,128)(2,1)}) custom-call(s32[16]{0:T(128)} %iota_xor_fusion.partner_ref, f32[16,32,128]{2,1,0:T(8,128)} %copy-done.4, f32[16,32,128]{2,1,0:T(8,128)} %copy-done.24, f32[16,32,128]{2,1,0:T(8,128)} %copy-done.23, f32[1,384]{1,0:T(1,128)} %bitcast.34, f32[1,384]{1,0:T(1,128)} %bitcast.35), custom_call_target="tpu_custom_call" | custom-call | flops 5000000000 | bytes 5000000 | tf_op jit(solution)/shard_map/weight/pallas_call | solution.py:299
  101.1 5.1 %analysis.1 = (f32[32,1024]{1,0:T(8,128)}, f32[32,1024]{1,0:T(8,128)}, f32[32,1024]{1,0:T(8,128)}, f32[32,1024]{1,0:T(8,128)}, f32[32,1024]{1,0:T(8,128)}, /*ind...) custom-call(bf16[512,512]{1,0:T(8,128)(2,1)} %get-tuple-element.42.h, ...), custom_call_target="tpu_custom_call" | custom-call | flops 1000000000 | bytes 5000000 | tf_op jit(solution)/shard_map/analysis/pallas_call | solution.py:311
  106.2 23.6 %collective-permute-start.4 = (f32[32,1024]{1,0:T(8,128)}, f32[32,1024]{1,0:T(8,128)S(1)}, u32[]{:S(2)}, u32[]{:S(2)}) collective-permute-start(f32[32,1024]{1,0:T(8,128)} %get-tuple-element.46), channel_id=1, source_target_pairs={{0,2},{2,0},{4,6},{6,4},{8,10},{10,8},{12,14},{14,12},{16,18},{18,... | collective-permute-start | bytes 393224 | tf_op jit(solution)/shard_map/ppermute | solution.py:324
  129.7 1.5 collective-permute-start.6
  131.3 3.4 %collective-permute-start.8 = (f32[32,1024]{1,0:T(8,128)}, f32[32,1024]{1,0:T(8,128)S(1)}, u32[]{:S(2)}, u32[]{:S(2)}) collective-permute-start(f32[32,1024]{1,0:T(8,128)} %get-tuple-element.50), channel_id=1, source_target_pairs={{0,10},{2,8},{4,14},{6,12},{8,2},{10,0},{12,6},{14,4},{16,26},{18,... | collective-permute-start | bytes 393224 | tf_op jit(solution)/shard_map/ppermute | solution.py:324
  134.7 1.5 collective-permute-done.5.rest_2_
  136.2 3.3 %collective-permute-start.10 = (f32[32,1024]{1,0:T(8,128)}, f32[32,1024]{1,0:T(8,128)S(1)}, u32[]{:S(2)}, u32[]{:S(2)}) collective-permute-start(f32[32,1024]{1,0:T(8,128)} %get-tuple-element.52), channel_id=1, source_target_pairs={{0,14},{2,12},{4,10},{6,8},{8,6},{10,4},{12,2},{14,0},{16,30},{18,... | collective-permute-start | bytes 393224 | tf_op jit(solution)/shard_map/ppermute | solution.py:324
  139.8 1.6 collective-permute-start.12
  142.1 6.3 %collective-permute-start.13 = (f32[32,1024]{1,0:T(8,128)}, f32[32,1024]{1,0:T(8,128)S(1)}, u32[]{:S(2)}, u32[]{:S(2)}) collective-permute-start(f32[32,1024]{1,0:T(8,128)} %get-tuple-element.55), channel_id=1, source_target_pairs={{0,20},{2,22},{4,16},{6,18},{8,28},{10,30},{12,24},{14,26},{16,4},... | collective-permute-start | bytes 393224 | tf_op jit(solution)/shard_map/ppermute | solution.py:324
  148.3 3.5 %collective-permute-start.14 = (f32[32,1024]{1,0:T(8,128)}, f32[32,1024]{1,0:T(8,128)S(1)}, u32[]{:S(2)}, u32[]{:S(2)}) collective-permute-start(f32[32,1024]{1,0:T(8,128)} %get-tuple-element.56), channel_id=1, source_target_pairs={{0,22},{2,20},{4,18},{6,16},{8,30},{10,28},{12,26},{14,24},{16,6},... | collective-permute-start | bytes 393224 | tf_op jit(solution)/shard_map/ppermute | solution.py:324
  151.8 10.0 %collective-permute-done.11.rest_8_ = f32[32,1024]{1,0:T(8,128)S(1)} collective-permute-done((f32[32,1024]{1,0:T(8,128)}, f32[32,1024]{1,0:T(8,128)S(1)}, u32[]{:S(2)}, u32[]{:S(2)}) %collective-permute-start.11) | collective-permute-done | bytes 131104 | tf_op jit(solution)/shard_map/ppermute | solution.py:324
  161.9 2.9 %collective-permute-done.12.rest_9_ = f32[32,1024]{1,0:T(8,128)S(1)} collective-permute-done((f32[32,1024]{1,0:T(8,128)}, f32[32,1024]{1,0:T(8,128)S(1)}, u32[]{:S(2)}, u32[]{:S(2)}) %collective-permute-start.12) | collective-permute-done | bytes 131104 | tf_op jit(solution)/shard_map/ppermute | solution.py:324
  164.9 4.0 %collective-permute-done.13.rest_10_ = f32[32,1024]{1,0:T(8,128)S(1)} collective-permute-done((f32[32,1024]{1,0:T(8,128)}, f32[32,1024]{1,0:T(8,128)S(1)}, u32[]{:S(2)}, u32[]{:S(2)}) %collective-permute-start.13) | collective-permute-done | bytes 131104 | tf_op jit(solution)/shard_map/ppermute | solution.py:324
  168.9 2.2 %collective-permute-start.18 = (f32[32,1024]{1,0:T(8,128)}, f32[32,1024]{1,0:T(8,128)S(1)}, u32[]{:S(2)}, u32[]{:S(2)}) collective-permute-start(f32[32,1024]{1,0:T(8,128)} %get-tuple-element.60), channel_id=1, source_target_pairs={{0,30},{2,28},{4,26},{6,24},{8,22},{10,20},{12,18},{14,16},{16,14}... | collective-permute-start | bytes 393224 | tf_op jit(solution)/shard_map/ppermute | solution.py:324
  171.8 5.6 %collective-permute-done.15.rest_12_ = f32[32,1024]{1,0:T(8,128)S(1)} collective-permute-done((f32[32,1024]{1,0:T(8,128)}, f32[32,1024]{1,0:T(8,128)S(1)}, u32[]{:S(2)}, u32[]{:S(2)}) %collective-permute-start.15) | collective-permute-done | bytes 131104 | tf_op jit(solution)/shard_map/ppermute | solution.py:324
  177.4 4.3 %collective-permute-done.16.rest_13_ = f32[32,1024]{1,0:T(8,128)S(1)} collective-permute-done((f32[32,1024]{1,0:T(8,128)}, f32[32,1024]{1,0:T(8,128)S(1)}, u32[]{:S(2)}, u32[]{:S(2)}) %collective-permute-start.16) | collective-permute-done | bytes 131104 | tf_op jit(solution)/shard_map/ppermute | solution.py:324
  181.8 2.3 %collective-permute-done.17.rest_14_ = f32[32,1024]{1,0:T(8,128)S(1)} collective-permute-done((f32[32,1024]{1,0:T(8,128)}, f32[32,1024]{1,0:T(8,128)S(1)}, u32[]{:S(2)}, u32[]{:S(2)}) %collective-permute-start.17) | collective-permute-done | bytes 131104 | tf_op jit(solution)/shard_map/ppermute | solution.py:324
  184.1 1.9 collective-permute-done.18.rest_15_
  186.7 6.5 %assemble.1 = f32[32,64,256]{2,1,0:T(8,128)} custom-call(s32[16]{0:T(128)} %iota_xor_fusion.partner_ref, f32[32,1024]{1,0:T(8,128)} %get-tuple-element.45.rest_0_, f32[32,1024]{1,0:T(8,128)} %copy-done.5, f32[32,1024]{1,0:T(8,128)} %copy-done.6, f32[32,1024]{1,0:T(8,128)} %copy-done.7, f32[32,1024]{1,0:T(8,128)} %copy-done.8, f32[32,1024]{1,0:T(8,128)} %copy-done.9, ...), custom_call_target="tpu_custom_call" | custom-call | flops 1000000 | bytes 5000000 | tf_op jit(solution)/shard_map/assemble/pallas_call | solution.py:325
  (86 shorter events, 15.3 us)
Async XLA Ops:
  2.6 1.6 collective-permute-start
  2.7 1.9 %collective-permute-start.1 = (f32[35,8,256]{2,1,0:T(8,128)S(1)}, f32[35,8,256]{2,1,0:T(8,128)S(1)}, u32[]{:S(2)}, u32[]{:S(2)}) collective-permute-start(f32[35,8,256]{2,1,0:T(8,128)S(1)} %pad_maximum_fusion.1), channel_id=1, source_target_pairs={{1,0},{0,1},{3,2},{2,3},{5,4},{4,5},{7,6},{6,7},{9,8},{8,9},{11,10... | collective-permute-start | bytes 860168 | tf_op jit(solution)/shard_map/ppermute | solution.py:269
  40.0 59.8 %all-to-all-start.1 = ((f32[16,32,1024]{2,1,0:T(8,128)}), f32[16,32,1024]{2,1,0:T(8,128)S(1)}, u32[]{:S(2)}, u32[]{:S(2)}) async-start(f32[16,32,1024]{2,1,0:T(8,128)} %get-tuple-element.44), calls=%async_computation.1 | async-start | bytes 4194304 | tf_op jit(solution)/shard_map/all_to_all | solution.py:297
  47.7 17.4 %collective-permute-start.3 = (f32[16,32,128]{2,1,0:T(8,128)S(1)}, f32[16,32,128]{2,1,0:T(8,128)S(1)}, u32[]{:S(2)}, u32[]{:S(2)}) collective-permute-start(f32[16,32,128]{2,1,0:T(8,128)S(1)} %all_to_all.10.own_ref), channel_id=1, source_target_pairs={{2,0},{4,2},{6,4},{8,6},{10,8},{12,10},{14,12},{16,14},{18,16},{20... | collective-permute-start | bytes 786440 | tf_op jit(solution)/shard_map/ppermute | solution.py:296
  49.2 26.1 %collective-permute-start.2 = (f32[16,32,128]{2,1,0:T(8,128)S(1)}, f32[16,32,128]{2,1,0:T(8,128)S(1)}, u32[]{:S(2)}, u32[]{:S(2)}) collective-permute-start(f32[16,32,128]{2,1,0:T(8,128)S(1)} %all_to_all.10.own_ref), channel_id=1, source_target_pairs={{0,2},{2,4},{4,6},{6,8},{8,10},{10,12},{12,14},{14,16},{16,18},{18... | collective-permute-start | bytes 786440 | tf_op jit(solution)/shard_map/ppermute | solution.py:295
  106.2 28.5 %collective-permute-start.4 = (f32[32,1024]{1,0:T(8,128)}, f32[32,1024]{1,0:T(8,128)S(1)}, u32[]{:S(2)}, u32[]{:S(2)}) collective-permute-start(f32[32,1024]{1,0:T(8,128)} %get-tuple-element.46), channel_id=1, source_target_pairs={{0,2},{2,0},{4,6},{6,4},{8,10},{10,8},{12,14},{14,12},{16,18},{18,... | collective-permute-start | bytes 393224 | tf_op jit(solution)/shard_map/ppermute | solution.py:324
  129.7 6.5 %collective-permute-start.5 = (f32[32,1024]{1,0:T(8,128)}, f32[32,1024]{1,0:T(8,128)S(1)}, u32[]{:S(2)}, u32[]{:S(2)}) collective-permute-start(f32[32,1024]{1,0:T(8,128)} %get-tuple-element.47), channel_id=1, source_target_pairs={{0,4},{2,6},{4,0},{6,2},{8,12},{10,14},{12,8},{14,10},{16,20},{18,... | collective-permute-start | bytes 393224 | tf_op jit(solution)/shard_map/ppermute | solution.py:324
  129.7 9.8 %collective-permute-start.6 = (f32[32,1024]{1,0:T(8,128)}, f32[32,1024]{1,0:T(8,128)S(1)}, u32[]{:S(2)}, u32[]{:S(2)}) collective-permute-start(f32[32,1024]{1,0:T(8,128)} %get-tuple-element.48), channel_id=1, source_target_pairs={{0,6},{2,4},{4,2},{6,0},{8,14},{10,12},{12,10},{14,8},{16,22},{18,... | collective-permute-start | bytes 393224 | tf_op jit(solution)/shard_map/ppermute | solution.py:324
  131.3 8.5 %collective-permute-start.7 = (f32[32,1024]{1,0:T(8,128)}, f32[32,1024]{1,0:T(8,128)S(1)}, u32[]{:S(2)}, u32[]{:S(2)}) collective-permute-start(f32[32,1024]{1,0:T(8,128)} %get-tuple-element.49), channel_id=1, source_target_pairs={{0,8},{2,10},{4,12},{6,14},{8,0},{10,2},{12,4},{14,6},{16,24},{18,... | collective-permute-start | bytes 393224 | tf_op jit(solution)/shard_map/ppermute | solution.py:324
  131.3 10.8 %collective-permute-start.8 = (f32[32,1024]{1,0:T(8,128)}, f32[32,1024]{1,0:T(8,128)S(1)}, u32[]{:S(2)}, u32[]{:S(2)}) collective-permute-start(f32[32,1024]{1,0:T(8,128)} %get-tuple-element.50), channel_id=1, source_target_pairs={{0,10},{2,8},{4,14},{6,12},{8,2},{10,0},{12,6},{14,4},{16,26},{18,... | collective-permute-start | bytes 393224 | tf_op jit(solution)/shard_map/ppermute | solution.py:324
  134.7 51.4 %copy-start.5 = (f32[32,1024]{1,0:T(8,128)}, f32[32,1024]{1,0:T(8,128)S(1)}, u32[]{:S(2)}) copy-start(f32[32,1024]{1,0:T(8,128)S(1)} %collective-permute-done.4.rest_1_) | copy-start | bytes 393220
  134.7 13.6 %collective-permute-start.9 = (f32[32,1024]{1,0:T(8,128)}, f32[32,1024]{1,0:T(8,128)S(1)}, u32[]{:S(2)}, u32[]{:S(2)}) collective-permute-start(f32[32,1024]{1,0:T(8,128)} %get-tuple-element.51), channel_id=1, source_target_pairs={{0,12},{2,14},{4,8},{6,10},{8,4},{10,6},{12,0},{14,2},{16,28},{18,... | collective-permute-start | bytes 393224 | tf_op jit(solution)/shard_map/ppermute | solution.py:324
  136.2 49.8 %copy-start.6 = (f32[32,1024]{1,0:T(8,128)}, f32[32,1024]{1,0:T(8,128)S(1)}, u32[]{:S(2)}) copy-start(f32[32,1024]{1,0:T(8,128)S(1)} %collective-permute-done.5.rest_2_) | copy-start | bytes 393220
  136.2 15.6 %collective-permute-start.10 = (f32[32,1024]{1,0:T(8,128)}, f32[32,1024]{1,0:T(8,128)S(1)}, u32[]{:S(2)}, u32[]{:S(2)}) collective-permute-start(f32[32,1024]{1,0:T(8,128)} %get-tuple-element.52), channel_id=1, source_target_pairs={{0,14},{2,12},{4,10},{6,8},{8,6},{10,4},{12,2},{14,0},{16,30},{18,... | collective-permute-start | bytes 393224 | tf_op jit(solution)/shard_map/ppermute | solution.py:324
  139.5 46.5 %copy-start.7 = (f32[32,1024]{1,0:T(8,128)}, f32[32,1024]{1,0:T(8,128)S(1)}, u32[]{:S(2)}) copy-start(f32[32,1024]{1,0:T(8,128)S(1)} %collective-permute-done.6.rest_3_) | copy-start | bytes 393220
  139.5 22.3 %collective-permute-start.11 = (f32[32,1024]{1,0:T(8,128)}, f32[32,1024]{1,0:T(8,128)S(1)}, u32[]{:S(2)}, u32[]{:S(2)}) collective-permute-start(f32[32,1024]{1,0:T(8,128)} %get-tuple-element.53), channel_id=1, source_target_pairs={{0,16},{2,18},{4,20},{6,22},{8,24},{10,26},{12,28},{14,30},{16,0},... | collective-permute-start | bytes 393224 | tf_op jit(solution)/shard_map/ppermute | solution.py:324
  139.8 46.2 %copy-start.8 = (f32[32,1024]{1,0:T(8,128)}, f32[32,1024]{1,0:T(8,128)S(1)}, u32[]{:S(2)}) copy-start(f32[32,1024]{1,0:T(8,128)S(1)} %collective-permute-done.7.rest_4_) | copy-start | bytes 393220
  139.8 25.0 %collective-permute-start.12 = (f32[32,1024]{1,0:T(8,128)}, f32[32,1024]{1,0:T(8,128)S(1)}, u32[]{:S(2)}, u32[]{:S(2)}) collective-permute-start(f32[32,1024]{1,0:T(8,128)} %get-tuple-element.54), channel_id=1, source_target_pairs={{0,18},{2,16},{4,22},{6,20},{8,26},{10,24},{12,30},{14,28},{16,2},... | collective-permute-start | bytes 393224 | tf_op jit(solution)/shard_map/ppermute | solution.py:324
  142.1 26.8 %collective-permute-start.13 = (f32[32,1024]{1,0:T(8,128)}, f32[32,1024]{1,0:T(8,128)S(1)}, u32[]{:S(2)}, u32[]{:S(2)}) collective-permute-start(f32[32,1024]{1,0:T(8,128)} %get-tuple-element.55), channel_id=1, source_target_pairs={{0,20},{2,22},{4,16},{6,18},{8,28},{10,30},{12,24},{14,26},{16,4},... | collective-permute-start | bytes 393224 | tf_op jit(solution)/shard_map/ppermute | solution.py:324
  148.3 23.5 %collective-permute-start.14 = (f32[32,1024]{1,0:T(8,128)}, f32[32,1024]{1,0:T(8,128)S(1)}, u32[]{:S(2)}, u32[]{:S(2)}) collective-permute-start(f32[32,1024]{1,0:T(8,128)} %get-tuple-element.56), channel_id=1, source_target_pairs={{0,22},{2,20},{4,18},{6,16},{8,30},{10,28},{12,26},{14,24},{16,6},... | collective-permute-start | bytes 393224 | tf_op jit(solution)/shard_map/ppermute | solution.py:324
  151.8 25.6 %collective-permute-start.15 = (f32[32,1024]{1,0:T(8,128)}, f32[32,1024]{1,0:T(8,128)S(1)}, u32[]{:S(2)}, u32[]{:S(2)}) collective-permute-start(f32[32,1024]{1,0:T(8,128)} %get-tuple-element.57), channel_id=1, source_target_pairs={{0,24},{2,26},{4,28},{6,30},{8,16},{10,18},{12,20},{14,22},{16,8},... | collective-permute-start | bytes 393224 | tf_op jit(solution)/shard_map/ppermute | solution.py:324
  161.8 19.9 %collective-permute-start.16 = (f32[32,1024]{1,0:T(8,128)}, f32[32,1024]{1,0:T(8,128)S(1)}, u32[]{:S(2)}, u32[]{:S(2)}) collective-permute-start(f32[32,1024]{1,0:T(8,128)} %get-tuple-element.58), channel_id=1, source_target_pairs={{0,26},{2,24},{4,30},{6,28},{8,18},{10,16},{12,22},{14,20},{16,10}... | collective-permute-start | bytes 393224 | tf_op jit(solution)/shard_map/ppermute | solution.py:324
  164.8 19.3 %collective-permute-start.17 = (f32[32,1024]{1,0:T(8,128)}, f32[32,1024]{1,0:T(8,128)S(1)}, u32[]{:S(2)}, u32[]{:S(2)}) collective-permute-start(f32[32,1024]{1,0:T(8,128)} %get-tuple-element.59), channel_id=1, source_target_pairs={{0,28},{2,30},{4,24},{6,26},{8,20},{10,22},{12,16},{14,18},{16,12}... | collective-permute-start | bytes 393224 | tf_op jit(solution)/shard_map/ppermute | solution.py:324
  168.9 17.2 %collective-permute-start.18 = (f32[32,1024]{1,0:T(8,128)}, f32[32,1024]{1,0:T(8,128)S(1)}, u32[]{:S(2)}, u32[]{:S(2)}) collective-permute-start(f32[32,1024]{1,0:T(8,128)} %get-tuple-element.60), channel_id=1, source_target_pairs={{0,30},{2,28},{4,26},{6,24},{8,22},{10,20},{12,18},{14,16},{16,14}... | collective-permute-start | bytes 393224 | tf_op jit(solution)/shard_map/ppermute | solution.py:324
  (21 other events, 299.0 us)
where the time goes:
time: 194 us; the launch traced here: 193 us
  waiting for transfers between devices  59.6 us (31%)
  Pallas kernels  54.1 us (28%)
  starting transfers between devices  54 us (28%)
  blocking collectives  15.8 us (8%)
  local copies, waits for them, and re-layouts  8.73 us (4%)
    ppermute x15, starting transfers between devices, body(): lax.ppermute(result[k], 'mem', [(i, i ^ k) for i in range(blocks)])  45.9 us
    ppermute x15, waiting for transfers between devices, body(): lax.ppermute(result[k], 'mem', [(i, i ^ k) for i in range(blocks)])  33.9 us
    pallas_call x1, Pallas kernels, body(): pl.pallas_call(weight_kernel, out_shape=[shape((size, size), BF16)] * 2,...  23.7 us
    pallas_call x1, Pallas kernels, body(): pl.pallas_call(functools.partial(forecast_kernel, blocks), out_shape=[sha...  18.9 us
    all_to_all x1, blocking collectives, body(): own = lax.all_to_all(seen, 'mem', 0, 0)  15.8 us
    ppermute x1, waiting for transfers between devices, body(): right = lax.ppermute(own, 'mem', [(j, i) for i, j in ring])  14.1 us
    ppermute x1, waiting for transfers between devices, body(): left = lax.ppermute(own, 'mem', ring)  10.2 us
    pallas_call x1, Pallas kernels, body(): pl.pallas_call(functools.partial(assemble_kernel, blocks), out_shape=shap...  6.47 us
  transfers between devices with their start and end apart: 20, of which 14 were waited for; matrix products, arithmetic and copies ran while one was open for 2% of the time, Pallas kernels for 12%

commit v1 on v0

--- a/solution.py
+++ b/solution.py
@@ -11,11 +11,13 @@
 PASSES = 6
 NS_ITERS = 8
 HALO = 8
-LINES = 16
+LINES = 36
+PARTS = 2
 F32 = jnp.float32
 BF16 = jnp.bfloat16
 VMEM = pl.BlockSpec(memory_space=pltpu.VMEM)
 SMEM = pl.BlockSpec(memory_space=pltpu.SMEM)
+HBM = pl.BlockSpec(memory_space=pltpu.HBM)
 
 
 def split(x):
@@ -45,8 +47,14 @@
     return rows
 
 
-def forecast_kernel(blocks, x_ref, up_ref, down_ref, av_ref, ah_ref, sp_ref, index_ref, fields, seen, one, two, coef):
+def forecast_kernel(x_hbm, up_ref, down_ref, av_ref, ah_ref, sp_ref, index_ref, *rest):
+    out, seen, x_ref, fields, one, two, coef, in_sems, out_sem = rest
+    blocks = fields.shape[0]
     members, rows, columns = x_ref.shape
+    loads = []
+    for m in range(0, members, 8):
+        loads.append(pltpu.make_async_copy(x_hbm.at[pl.ds(m, 8)], x_ref.at[pl.ds(m, 8)], in_sems.at[m // 8]))
+        loads[-1].start()
     total = rows + 2 * HALO
     width = columns // blocks
     per = 128 // width
@@ -56,13 +64,6 @@
         tile = source[pl.ds(member, 8), pl.ds(row, 8), :]
         one[pl.ds(target, 8), pl.ds(member, 8), :] = jnp.swapaxes(tile, 0, 1)
 
-    def load_rows(t, carry):
-        row = pl.multiple_of(t * 8, 8)
-        for m in range(0, members, 8):
-            place(x_ref, m, row, HALO + row)
-        return carry
-
-    lax.fori_loop(0, rows // 8, load_rows, 0)
     for m in range(0, members, 8):
         place(up_ref, m, 0, 0)
         place(down_ref, m, 0, HALO + rows)
@@ -81,6 +82,15 @@
         return carry
 
     lax.fori_loop(0, rows // 8, coef_rows, 0)
+    for m, load in zip(range(0, members, 8), loads):
+        load.wait()
+
+        def load_rows(t, carry, m=m):
+            row = pl.multiple_of(t * 8, 8)
+            place(x_ref, m, row, HALO + row)
+            return carry
+
+        lax.fori_loop(0, rows // 8, load_rows, 0)
 
     def wide(value):
         return jnp.concatenate([value] * (members // 8), axis=0)
@@ -117,15 +127,18 @@
     def cut(t, carry):
         row = HALO + t * per
         at = pl.multiple_of(t * 128, 128)
-        for h in range(columns // 128):
-            lines = [final[row + i, :, h * 128 : (h + 1) * 128] for i in range(per)]
-            for j, piece in enumerate(swap_granules(lines, lane, width)):
-                fields[h * per + j, :, pl.ds(at, 128)] = piece
+        for m in range(0, members, 8):
+            for h in range(columns // 128):
+                lines = [final[row + i, m : m + 8, h * 128 : (h + 1) * 128] for i in range(per)]
+                for j, piece in enumerate(swap_granules(lines, lane[:8], width)):
+                    fields[h * per + j, m : m + 8, pl.ds(at, 128)] = piece
         return carry
 
     lax.fori_loop(0, rows // per, cut, 0)
-
-    def look(b, carry):
+    store = pltpu.make_async_copy(fields, out, out_sem)
+    store.start()
+
+    def look_at(b):
         index = jnp.broadcast_to(index_ref[b], (members, 128))
         low, high = index % 128, index // 128
         value = jnp.zeros((members, 128), F32)
@@ -134,9 +147,14 @@
             picked = jnp.take_along_axis(part, low, axis=1, mode="promise_in_bounds")
             value = jnp.where(high == t, picked, value)
         seen[b] = value
-        return carry
-
-    lax.fori_loop(0, blocks, look, 0)
+
+    def look(t, carry):
+        for i in range(4):
+            look_at(4 * t + i)
+        return carry
+
+    lax.fori_loop(0, blocks // 4, look, 0)
+    store.wait()
 
 
 def weight_kernel(partner_ref, own_ref, left_ref, right_ref, prec_ref, value_ref, high_ref, low_ref, stacked, innovation, mh, ml, zh, zl, fh, fl):
@@ -188,20 +206,19 @@
 
 
 def analysis_kernel(high_ref, low_ref, fields, *rest):
-    outs, (ah, al, center) = rest[:-3], rest[-3:]
-    blocks, chunk, _ = fields.shape
+    outs, (ah, al) = rest[:-2], rest[-2:]
+    blocks, chunk = fields.shape[:2]
     size = blocks * chunk
     total = fields[0]
     for k in range(1, blocks):
         total = total + fields[k]
-    center[...] = jnp.sum(total, axis=0, keepdims=True) * (1.0 / size)
+    center = jnp.sum(total, axis=0, keepdims=True) * (1.0 / size)
     for k in range(blocks):
-        high, low = split(fields[k] - center[...])
-        ah[k * chunk : (k + 1) * chunk, :] = high
-        al[k * chunk : (k + 1) * chunk, :] = low
+        row = k * chunk
+        ah[row : row + chunk, :], al[row : row + chunk, :] = split(fields[k] - center)
     result = dot_split((high_ref[...], low_ref[...]), (ah[...], al[...]))
     for k in range(blocks):
-        outs[k][...] = result[k * chunk : (k + 1) * chunk, :] + center[...]
+        outs[k][...] = result[k * chunk : (k + 1) * chunk, :] + center
 
 
 def assemble_kernel(blocks, partner_ref, *rest):
@@ -237,6 +254,77 @@
 
 
 PARAMS = pltpu.CompilerParams(vmem_limit_bytes=56 * 1024 * 1024)
+
+
+def call_forecast(blocks, x, above, below, coefs, index):
+    members, rows, columns = x.shape
+    cells = rows * columns // blocks
+    return pl.pallas_call(
+        forecast_kernel,
+        out_shape=[shape((blocks, members, cells)), shape((blocks, members, index.shape[2]))],
+        in_specs=[HBM] + [VMEM] * 6,
+        out_specs=[HBM, VMEM],
+        scratch_shapes=[
+            pltpu.VMEM((members, rows, columns), F32),
+            pltpu.VMEM((blocks, members, cells), F32),
+            pltpu.VMEM((rows + 2 * HALO, members, columns), F32),
+            pltpu.VMEM((rows + 2 * HALO, members, columns), F32),
+            pltpu.VMEM((4, rows + 2 * HALO, 8, columns), F32),
+            pltpu.SemaphoreType.DMA((members // 8,)),
+            pltpu.SemaphoreType.DMA,
+        ],
+        compiler_params=PARAMS,
+        cost_estimate=cost(5e6, 5e6),
+        name="forecast",
+    )(x, above, below, *coefs, index)
+
+
+def call_weight(partner, own, left, right, precision, values):
+    blocks, members, nobs = own.shape
+    size = blocks * members
+    return pl.pallas_call(
+        weight_kernel,
+        out_shape=[shape((size, size), BF16)] * 2,
+        in_specs=[SMEM] + [VMEM] * 5,
+        out_specs=[VMEM] * 2,
+        scratch_shapes=[pltpu.VMEM((size, 3 * nobs), F32), pltpu.VMEM((1, 3 * nobs), F32)]
+        + [pltpu.VMEM((size, size), BF16)] * 6,
+        compiler_params=PARAMS,
+        cost_estimate=cost(5e9, 5e6),
+        name="weight",
+    )(partner, own, left, right, precision, values)
+
+
+def call_analysis(high, low, fields):
+    blocks, members, cells = fields.shape
+    size = blocks * members
+    whole = pl.BlockSpec((size, size), lambda i: (0, 0))
+    return pl.pallas_call(
+        analysis_kernel,
+        grid=(PARTS,),
+        out_shape=[shape((members, cells))] * blocks,
+        in_specs=[whole, whole, pl.BlockSpec((blocks, members, cells // PARTS), lambda i: (0, 0, i))],
+        out_specs=[pl.BlockSpec((members, cells // PARTS), lambda i: (0, i))] * blocks,
+        scratch_shapes=[pltpu.VMEM((size, cells // PARTS), BF16)] * 2,
+        compiler_params=PARAMS,
+        cost_estimate=cost(1e9, 5e6),
+        name="analysis",
+    )(high, low, fields)
+
+
+def call_assemble(partner, pieces, dims):
+    members, _, columns = dims
+    blocks = len(pieces)
+    return pl.pallas_call(
+        functools.partial(assemble_kernel, blocks),
+        out_shape=shape(dims),
+        in_specs=[SMEM] + [VMEM] * blocks,
+        out_specs=VMEM,
+        scratch_shapes=[pltpu.VMEM((blocks,) + pieces[0].shape, F32), pltpu.VMEM((8, members, columns), F32)],
+        compiler_params=PARAMS,
+        cost_estimate=cost(1e6, 5e6),
+        name="assemble",
+    )(partner, *pieces)
 
 
 def body(
@@ -253,9 +341,6 @@
     blocks = lax.axis_size("mem")
     tiles = lax.axis_size("tile")
     members, rows, columns = starting_samples.shape
-    nobs = obs_index.shape[2]
-    cells = rows * (columns // blocks)
-    size = blocks * members
     me = lax.axis_index("mem")
 
     coefs = (transport_number_vertical, transport_number_horizontal, spreading_number)
@@ -268,21 +353,12 @@
     above = lax.ppermute(edge(slice(rows - HALO, rows)), "tile", up)
     below = lax.ppermute(edge(slice(0, HALO)), "tile", down)
 
-    fields, seen = pl.pallas_call(
-        functools.partial(forecast_kernel, blocks),
-        out_shape=[shape((blocks, members, cells)), shape((blocks, members, nobs))],
-        in_specs=[VMEM] * 7,
-        out_specs=[VMEM] * 2,
-        scratch_shapes=[
-            pltpu.VMEM((rows + 2 * HALO, members, columns), F32),
-            pltpu.VMEM((rows + 2 * HALO, members, columns), F32),
-            pltpu.VMEM((4, rows + 2 * HALO, 8, columns), F32),
-        ],
-        compiler_params=PARAMS,
-        cost_estimate=cost(5e6, 5e6),
-        name="forecast",
-    )(starting_samples, above, below, *coefs, obs_index[0][:, None, :])
-
+    fields, seen = call_forecast(blocks, starting_samples, above, below, coefs, obs_index[0][:, None, :])
+
+    def swap(x, k):
+        return lax.ppermute(x, "mem", [(i, i ^ k) for i in range(blocks)])
+
+    ring = [(i, (i + 1) % blocks) for i in range(blocks)]
     seen, obs_value, obs_error, loc_index = lax.optimization_barrier((seen, obs_value, obs_error, loc_index))
     own = lax.all_to_all(seen, "mem", 0, 0)
     roles = (me + jnp.arange(3, dtype=jnp.int32) - 1) % blocks
@@ -291,47 +367,15 @@
     values = obs_value[0][roles]
     partner = jnp.bitwise_xor(me, jnp.arange(blocks, dtype=jnp.int32))
     own, precision, values, partner = lax.optimization_barrier((own, precision, values, partner))
-    ring = [(i, (i + 1) % blocks) for i in range(blocks)]
     left = lax.ppermute(own, "mem", ring)
     right = lax.ppermute(own, "mem", [(j, i) for i, j in ring])
     fields = lax.all_to_all(fields, "mem", 0, 0)
-
-    high, low = pl.pallas_call(
-        weight_kernel,
-        out_shape=[shape((size, size), BF16)] * 2,
-        in_specs=[SMEM] + [VMEM] * 5,
-        out_specs=[VMEM] * 2,
-        scratch_shapes=[pltpu.VMEM((size, 3 * nobs), F32), pltpu.VMEM((1, 3 * nobs), F32)]
-        + [pltpu.VMEM((size, size), BF16)] * 6,
-        compiler_params=PARAMS,
-        cost_estimate=cost(5e9, 5e6),
-        name="weight",
-    )(partner, own, left, right, precision.reshape(1, -1), values.reshape(1, -1))
-
-    result = pl.pallas_call(
-        analysis_kernel,
-        out_shape=[shape((members, cells))] * blocks,
-        in_specs=[VMEM] * 3,
-        out_specs=[VMEM] * blocks,
-        scratch_shapes=[pltpu.VMEM((size, cells), BF16)] * 2 + [pltpu.VMEM((1, cells), F32)],
-        compiler_params=PARAMS,
-        cost_estimate=cost(1e9, 5e6),
-        name="analysis",
-    )(high, low, fields)
-
+    high, low = call_weight(partner, own, left, right, precision.reshape(1, -1), values.reshape(1, -1))
+    result = call_analysis(high, low, fields)
     back = {0: result[0]}
-    for k in sorted(range(1, blocks), reverse=True):
-        back[k] = lax.ppermute(result[k], "mem", [(i, i ^ k) for i in range(blocks)])
-    return pl.pallas_call(
-        functools.partial(assemble_kernel, blocks),
-        out_shape=shape((members, rows, columns)),
-        in_specs=[SMEM] + [VMEM] * blocks,
-        out_specs=VMEM,
-        scratch_shapes=[pltpu.VMEM((blocks, members, cells), F32), pltpu.VMEM((8, members, columns), F32)],
-        compiler_params=PARAMS,
-        cost_estimate=cost(1e6, 5e6),
-        name="assemble",
-    )(partner, *[back[k] for k in range(blocks)])
+    for k in range(blocks - 1, 0, -1):
+        back[k] = swap(result[k], k)
+    return call_assemble(partner, [back[k] for k in range(blocks)], (members, rows, columns))
 
 
 def solution(mesh):

time: 194 us -> 191 us (0.985)
  Pallas kernels: 54.1 us -> 51.1 us
    pallas_call x4, Pallas kernels: 54.1 us -> 51.1 us  [the longest x1 23.7 us: call_weight(): pl.pallas_call(weight_kernel, out_shape=[shape((size, size), BF16)] * 2,...]
where the time goes in v1:
time: 191 us; the launch traced here: 190 us
  waiting for transfers between devices  59.6 us (31%)
  starting transfers between devices  54 us (28%)
  Pallas kernels  51.1 us (27%)
  blocking collectives  15.8 us (8%)
  local copies, waits for them, and re-layouts  8.73 us (5%)
    ppermute x15, starting transfers between devices, swap(): return lax.ppermute(x, 'mem', [(i, i ^ k) for i in range(blocks)])  46 us
    ppermute x15, waiting for transfers between devices, swap(): return lax.ppermute(x, 'mem', [(i, i ^ k) for i in range(blocks)])  33.9 us
    pallas_call x1, Pallas kernels, call_weight(): pl.pallas_call(weight_kernel, out_shape=[shape((size, size), BF16)] * 2,...  23.7 us
    pallas_call x1, Pallas kernels, call_forecast(): pl.pallas_call(forecast_kernel, out_shape=[shape((blocks, members, cells)...  16.3 us
    all_to_all x1, blocking collectives, body(): own = lax.all_to_all(seen, 'mem', 0, 0)  15.8 us
    ppermute x1, waiting for transfers between devices, body(): right = lax.ppermute(own, 'mem', [(j, i) for i, j in ring])  14.1 us
    ppermute x1, waiting for transfers between devices, body(): left = lax.ppermute(own, 'mem', ring)  10.2 us
    pallas_call x1, Pallas kernels, call_assemble(): pl.pallas_call(functools.partial(assemble_kernel, blocks), out_shape=shap...  6.47 us
  transfers between devices with their start and end apart: 20, of which 14 were waited for; matrix products, arithmetic and copies ran while one was open for 2% of the time, Pallas kernels for 12%

profile of v1, /device:TPU:12, one launch (start us, length us, event | category | flops | bytes accessed | tf_op | source)
XLA Modules:
  0.0 190.2 jit_solution(11670155475625144222)
XLA Ops:
  5.3 16.3 %forecast.1 = (f32[16,32,1024]{2,1,0:T(8,128)}, f32[16,32,128]{2,1,0:T(8,128)}) custom-call(f32[32,64,256]{2,1,0:T(8,128)} %x_hbm.1, f32[35,8,256]{2,1,0:T(8,128)} %copy-done.2, f32[35,8,256]{2,1,0:T(8,128)} %copy-done.3, f32[64,256]{1,0:T(8,128)} %av_ref.1, f32[64,256]{1,0:T(8,128)} %ah_ref.1, f32[64,256]{1,0:T(8,128)} %sp_ref.1, s32[16,1,128]{2,1,0:T(1,128)} %bitcast.31), custom_call_target="tpu_custom_call" | custom-call | flops 5000000 | bytes 5000000 | tf_op jit(solution)/shard_map/forecast/pallas_call | solution.py:262
  21.6 15.8 %all_to_all.10.own_ref = f32[16,32,128]{2,1,0:T(8,128)S(1)} all-to-all(f32[16,32,128]{2,1,0:T(8,128)} %get-tuple-element.34), channel_id=1, replica_groups=mesh['mem'=16,'tile'=2] {'mem'}, dimensions={0} | all-to-all | bytes 524288 | tf_op jit(solution)/shard_map/all_to_all | solution.py:363
  37.4 5.3 %all-to-all-start.1 = ((f32[16,32,1024]{2,1,0:T(8,128)}), f32[16,32,1024]{2,1,0:T(8,128)S(1)}, u32[]{:S(2)}, u32[]{:S(2)}) async-start(f32[16,32,1024]{2,1,0:T(8,128)} %get-tuple-element.44), calls=%async_computation.1 | async-start | bytes 4194304 | tf_op jit(solution)/shard_map/all_to_all | solution.py:372
  45.1 1.5 collective-permute-start.3
  48.4 14.1 %collective-permute-done.3.right_ref = f32[16,32,128]{2,1,0:T(8,128)S(1)} collective-permute-done((f32[16,32,128]{2,1,0:T(8,128)S(1)}, f32[16,32,128]{2,1,0:T(8,128)S(1)}, u32[]{:S(2)}, u32[]{:S(2)}) %collective-permute-start.3) | collective-permute-done | bytes 262176 | tf_op jit(solution)/shard_map/ppermute | solution.py:371
  62.5 10.2 %collective-permute-done.2.left_ref = f32[16,32,128]{2,1,0:T(8,128)S(1)} collective-permute-done((f32[16,32,128]{2,1,0:T(8,128)S(1)}, f32[16,32,128]{2,1,0:T(8,128)S(1)}, u32[]{:S(2)}, u32[]{:S(2)}) %collective-permute-start.2) | collective-permute-done | bytes 262176 | tf_op jit(solution)/shard_map/ppermute | solution.py:370
  73.5 23.7 %weight.1 = (bf16[512,512]{1,0:T(8,128)(2,1)}, bf16[512,512]{1,0:T(8,128)(2,1)}) custom-call(s32[16]{0:T(128)} %iota_xor_fusion.partner_ref, f32[16,32,128]{2,1,0:T(8,128)} %copy-done.4, f32[16,32,128]{2,1,0:T(8,128)} %copy-done.24, f32[16,32,128]{2,1,0:T(8,128)} %copy-done.23, f32[1,384]{1,0:T(1,128)} %bitcast.34, f32[1,384]{1,0:T(1,128)} %bitcast.35), custom_call_target="tpu_custom_call" | custom-call | flops 5000000000 | bytes 5000000 | tf_op jit(solution)/shard_map/weight/pallas_call | solution.py:285
  98.5 4.7 %analysis.1 = (f32[32,1024]{1,0:T(8,128)}, f32[32,1024]{1,0:T(8,128)}, f32[32,1024]{1,0:T(8,128)}, f32[32,1024]{1,0:T(8,128)}, f32[32,1024]{1,0:T(8,128)}, /*ind...) custom-call(bf16[512,512]{1,0:T(8,128)(2,1)} %get-tuple-element.42.h, ...), custom_call_target="tpu_custom_call" | custom-call | flops 1000000000 | bytes 5000000 | tf_op jit(solution)/shard_map/analysis/pallas_call | solution.py:302
  103.2 23.6 %collective-permute-start.4 = (f32[32,1024]{1,0:T(8,128)}, f32[32,1024]{1,0:T(8,128)S(1)}, u32[]{:S(2)}, u32[]{:S(2)}) collective-permute-start(f32[32,1024]{1,0:T(8,128)} %get-tuple-element.46), channel_id=1, source_target_pairs={{0,2},{2,0},{4,6},{6,4},{8,10},{10,8},{12,14},{14,12},{16,18},{18,... | collective-permute-start | bytes 393224 | tf_op jit(solution)/shard_map/ppermute | solution.py:359
  126.8 1.5 collective-permute-start.6
  128.4 3.4 %collective-permute-start.8 = (f32[32,1024]{1,0:T(8,128)}, f32[32,1024]{1,0:T(8,128)S(1)}, u32[]{:S(2)}, u32[]{:S(2)}) collective-permute-start(f32[32,1024]{1,0:T(8,128)} %get-tuple-element.50), channel_id=1, source_target_pairs={{0,10},{2,8},{4,14},{6,12},{8,2},{10,0},{12,6},{14,4},{16,26},{18,... | collective-permute-start | bytes 393224 | tf_op jit(solution)/shard_map/ppermute | solution.py:359
  133.3 3.3 %collective-permute-start.10 = (f32[32,1024]{1,0:T(8,128)}, f32[32,1024]{1,0:T(8,128)S(1)}, u32[]{:S(2)}, u32[]{:S(2)}) collective-permute-start(f32[32,1024]{1,0:T(8,128)} %get-tuple-element.52), channel_id=1, source_target_pairs={{0,14},{2,12},{4,10},{6,8},{8,6},{10,4},{12,2},{14,0},{16,30},{18,... | collective-permute-start | bytes 393224 | tf_op jit(solution)/shard_map/ppermute | solution.py:359
  136.9 1.6 collective-permute-start.12
  139.2 6.3 %collective-permute-start.13 = (f32[32,1024]{1,0:T(8,128)}, f32[32,1024]{1,0:T(8,128)S(1)}, u32[]{:S(2)}, u32[]{:S(2)}) collective-permute-start(f32[32,1024]{1,0:T(8,128)} %get-tuple-element.55), channel_id=1, source_target_pairs={{0,20},{2,22},{4,16},{6,18},{8,28},{10,30},{12,24},{14,26},{16,4},... | collective-permute-start | bytes 393224 | tf_op jit(solution)/shard_map/ppermute | solution.py:359
  145.4 3.4 %collective-permute-start.14 = (f32[32,1024]{1,0:T(8,128)}, f32[32,1024]{1,0:T(8,128)S(1)}, u32[]{:S(2)}, u32[]{:S(2)}) collective-permute-start(f32[32,1024]{1,0:T(8,128)} %get-tuple-element.56), channel_id=1, source_target_pairs={{0,22},{2,20},{4,18},{6,16},{8,30},{10,28},{12,26},{14,24},{16,6},... | collective-permute-start | bytes 393224 | tf_op jit(solution)/shard_map/ppermute | solution.py:359
  148.8 10.1 %collective-permute-done.11.rest_8_ = f32[32,1024]{1,0:T(8,128)S(1)} collective-permute-done((f32[32,1024]{1,0:T(8,128)}, f32[32,1024]{1,0:T(8,128)S(1)}, u32[]{:S(2)}, u32[]{:S(2)}) %collective-permute-start.11) | collective-permute-done | bytes 131104 | tf_op jit(solution)/shard_map/ppermute | solution.py:359
  159.0 2.9 %collective-permute-done.12.rest_9_ = f32[32,1024]{1,0:T(8,128)S(1)} collective-permute-done((f32[32,1024]{1,0:T(8,128)}, f32[32,1024]{1,0:T(8,128)S(1)}, u32[]{:S(2)}, u32[]{:S(2)}) %collective-permute-start.12) | collective-permute-done | bytes 131104 | tf_op jit(solution)/shard_map/ppermute | solution.py:359
  162.0 4.0 %collective-permute-done.13.rest_10_ = f32[32,1024]{1,0:T(8,128)S(1)} collective-permute-done((f32[32,1024]{1,0:T(8,128)}, f32[32,1024]{1,0:T(8,128)S(1)}, u32[]{:S(2)}, u32[]{:S(2)}) %collective-permute-start.13) | collective-permute-done | bytes 131104 | tf_op jit(solution)/shard_map/ppermute | solution.py:359
  166.0 2.2 %collective-permute-start.18 = (f32[32,1024]{1,0:T(8,128)}, f32[32,1024]{1,0:T(8,128)S(1)}, u32[]{:S(2)}, u32[]{:S(2)}) collective-permute-start(f32[32,1024]{1,0:T(8,128)} %get-tuple-element.60), channel_id=1, source_target_pairs={{0,30},{2,28},{4,26},{6,24},{8,22},{10,20},{12,18},{14,16},{16,14}... | collective-permute-start | bytes 393224 | tf_op jit(solution)/shard_map/ppermute | solution.py:359
  168.9 5.6 %collective-permute-done.15.rest_12_ = f32[32,1024]{1,0:T(8,128)S(1)} collective-permute-done((f32[32,1024]{1,0:T(8,128)}, f32[32,1024]{1,0:T(8,128)S(1)}, u32[]{:S(2)}, u32[]{:S(2)}) %collective-permute-start.15) | collective-permute-done | bytes 131104 | tf_op jit(solution)/shard_map/ppermute | solution.py:359
  174.5 4.3 %collective-permute-done.16.rest_13_ = f32[32,1024]{1,0:T(8,128)S(1)} collective-permute-done((f32[32,1024]{1,0:T(8,128)}, f32[32,1024]{1,0:T(8,128)S(1)}, u32[]{:S(2)}, u32[]{:S(2)}) %collective-permute-start.16) | collective-permute-done | bytes 131104 | tf_op jit(solution)/shard_map/ppermute | solution.py:359
  178.9 2.3 %collective-permute-done.17.rest_14_ = f32[32,1024]{1,0:T(8,128)S(1)} collective-permute-done((f32[32,1024]{1,0:T(8,128)}, f32[32,1024]{1,0:T(8,128)S(1)}, u32[]{:S(2)}, u32[]{:S(2)}) %collective-permute-start.17) | collective-permute-done | bytes 131104 | tf_op jit(solution)/shard_map/ppermute | solution.py:359
  181.1 2.0 %collective-permute-done.18.rest_15_ = f32[32,1024]{1,0:T(8,128)S(1)} collective-permute-done((f32[32,1024]{1,0:T(8,128)}, f32[32,1024]{1,0:T(8,128)S(1)}, u32[]{:S(2)}, u32[]{:S(2)}) %collective-permute-start.18) | collective-permute-done | bytes 131104 | tf_op jit(solution)/shard_map/ppermute | solution.py:359
  183.8 6.5 %assemble.1 = f32[32,64,256]{2,1,0:T(8,128)} custom-call(s32[16]{0:T(128)} %iota_xor_fusion.partner_ref, f32[32,1024]{1,0:T(8,128)} %get-tuple-element.45.rest_0_, f32[32,1024]{1,0:T(8,128)} %copy-done.5, f32[32,1024]{1,0:T(8,128)} %copy-done.6, f32[32,1024]{1,0:T(8,128)} %copy-done.7, f32[32,1024]{1,0:T(8,128)} %copy-done.8, f32[32,1024]{1,0:T(8,128)} %copy-done.9, ...), custom_call_target="tpu_custom_call" | custom-call | flops 1000000 | bytes 5000000 | tf_op jit(solution)/shard_map/assemble/pallas_call | solution.py:318
  (86 shorter events, 15.3 us)
Async XLA Ops:
  2.6 1.6 collective-permute-start
  2.7 1.9 %collective-permute-start.1 = (f32[35,8,256]{2,1,0:T(8,128)S(1)}, f32[35,8,256]{2,1,0:T(8,128)S(1)}, u32[]{:S(2)}, u32[]{:S(2)}) collective-permute-start(f32[35,8,256]{2,1,0:T(8,128)S(1)} %pad_maximum_fusion.1), channel_id=1, source_target_pairs={{1,0},{0,1},{3,2},{2,3},{5,4},{4,5},{7,6},{6,7},{9,8},{8,9},{11,10... | collective-permute-start | bytes 860168 | tf_op jit(solution)/shard_map/ppermute | solution.py:354
  37.4 59.7 %all-to-all-start.1 = ((f32[16,32,1024]{2,1,0:T(8,128)}), f32[16,32,1024]{2,1,0:T(8,128)S(1)}, u32[]{:S(2)}, u32[]{:S(2)}) async-start(f32[16,32,1024]{2,1,0:T(8,128)} %get-tuple-element.44), calls=%async_computation.1 | async-start | bytes 4194304 | tf_op jit(solution)/shard_map/all_to_all | solution.py:372
  45.1 17.4 %collective-permute-start.3 = (f32[16,32,128]{2,1,0:T(8,128)S(1)}, f32[16,32,128]{2,1,0:T(8,128)S(1)}, u32[]{:S(2)}, u32[]{:S(2)}) collective-permute-start(f32[16,32,128]{2,1,0:T(8,128)S(1)} %all_to_all.10.own_ref), channel_id=1, source_target_pairs={{2,0},{4,2},{6,4},{8,6},{10,8},{12,10},{14,12},{16,14},{18,16},{20... | collective-permute-start | bytes 786440 | tf_op jit(solution)/shard_map/ppermute | solution.py:371
  46.7 26.1 %collective-permute-start.2 = (f32[16,32,128]{2,1,0:T(8,128)S(1)}, f32[16,32,128]{2,1,0:T(8,128)S(1)}, u32[]{:S(2)}, u32[]{:S(2)}) collective-permute-start(f32[16,32,128]{2,1,0:T(8,128)S(1)} %all_to_all.10.own_ref), channel_id=1, source_target_pairs={{0,2},{2,4},{4,6},{6,8},{8,10},{10,12},{12,14},{14,16},{16,18},{18... | collective-permute-start | bytes 786440 | tf_op jit(solution)/shard_map/ppermute | solution.py:370
  103.2 28.6 %collective-permute-start.4 = (f32[32,1024]{1,0:T(8,128)}, f32[32,1024]{1,0:T(8,128)S(1)}, u32[]{:S(2)}, u32[]{:S(2)}) collective-permute-start(f32[32,1024]{1,0:T(8,128)} %get-tuple-element.46), channel_id=1, source_target_pairs={{0,2},{2,0},{4,6},{6,4},{8,10},{10,8},{12,14},{14,12},{16,18},{18,... | collective-permute-start | bytes 393224 | tf_op jit(solution)/shard_map/ppermute | solution.py:359
  126.8 6.5 %collective-permute-start.5 = (f32[32,1024]{1,0:T(8,128)}, f32[32,1024]{1,0:T(8,128)S(1)}, u32[]{:S(2)}, u32[]{:S(2)}) collective-permute-start(f32[32,1024]{1,0:T(8,128)} %get-tuple-element.47), channel_id=1, source_target_pairs={{0,4},{2,6},{4,0},{6,2},{8,12},{10,14},{12,8},{14,10},{16,20},{18,... | collective-permute-start | bytes 393224 | tf_op jit(solution)/shard_map/ppermute | solution.py:359
  126.8 9.8 %collective-permute-start.6 = (f32[32,1024]{1,0:T(8,128)}, f32[32,1024]{1,0:T(8,128)S(1)}, u32[]{:S(2)}, u32[]{:S(2)}) collective-permute-start(f32[32,1024]{1,0:T(8,128)} %get-tuple-element.48), channel_id=1, source_target_pairs={{0,6},{2,4},{4,2},{6,0},{8,14},{10,12},{12,10},{14,8},{16,22},{18,... | collective-permute-start | bytes 393224 | tf_op jit(solution)/shard_map/ppermute | solution.py:359
  128.4 8.5 %collective-permute-start.7 = (f32[32,1024]{1,0:T(8,128)}, f32[32,1024]{1,0:T(8,128)S(1)}, u32[]{:S(2)}, u32[]{:S(2)}) collective-permute-start(f32[32,1024]{1,0:T(8,128)} %get-tuple-element.49), channel_id=1, source_target_pairs={{0,8},{2,10},{4,12},{6,14},{8,0},{10,2},{12,4},{14,6},{16,24},{18,... | collective-permute-start | bytes 393224 | tf_op jit(solution)/shard_map/ppermute | solution.py:359
  128.4 10.8 %collective-permute-start.8 = (f32[32,1024]{1,0:T(8,128)}, f32[32,1024]{1,0:T(8,128)S(1)}, u32[]{:S(2)}, u32[]{:S(2)}) collective-permute-start(f32[32,1024]{1,0:T(8,128)} %get-tuple-element.50), channel_id=1, source_target_pairs={{0,10},{2,8},{4,14},{6,12},{8,2},{10,0},{12,6},{14,4},{16,26},{18,... | collective-permute-start | bytes 393224 | tf_op jit(solution)/shard_map/ppermute | solution.py:359
  131.8 51.3 %copy-start.5 = (f32[32,1024]{1,0:T(8,128)}, f32[32,1024]{1,0:T(8,128)S(1)}, u32[]{:S(2)}) copy-start(f32[32,1024]{1,0:T(8,128)S(1)} %collective-permute-done.4.rest_1_) | copy-start | bytes 393220
  131.8 13.6 %collective-permute-start.9 = (f32[32,1024]{1,0:T(8,128)}, f32[32,1024]{1,0:T(8,128)S(1)}, u32[]{:S(2)}, u32[]{:S(2)}) collective-permute-start(f32[32,1024]{1,0:T(8,128)} %get-tuple-element.51), channel_id=1, source_target_pairs={{0,12},{2,14},{4,8},{6,10},{8,4},{10,6},{12,0},{14,2},{16,28},{18,... | collective-permute-start | bytes 393224 | tf_op jit(solution)/shard_map/ppermute | solution.py:359
  133.3 49.8 %copy-start.6 = (f32[32,1024]{1,0:T(8,128)}, f32[32,1024]{1,0:T(8,128)S(1)}, u32[]{:S(2)}) copy-start(f32[32,1024]{1,0:T(8,128)S(1)} %collective-permute-done.5.rest_2_) | copy-start | bytes 393220
  133.3 15.6 %collective-permute-start.10 = (f32[32,1024]{1,0:T(8,128)}, f32[32,1024]{1,0:T(8,128)S(1)}, u32[]{:S(2)}, u32[]{:S(2)}) collective-permute-start(f32[32,1024]{1,0:T(8,128)} %get-tuple-element.52), channel_id=1, source_target_pairs={{0,14},{2,12},{4,10},{6,8},{8,6},{10,4},{12,2},{14,0},{16,30},{18,... | collective-permute-start | bytes 393224 | tf_op jit(solution)/shard_map/ppermute | solution.py:359
  136.6 46.5 %copy-start.7 = (f32[32,1024]{1,0:T(8,128)}, f32[32,1024]{1,0:T(8,128)S(1)}, u32[]{:S(2)}) copy-start(f32[32,1024]{1,0:T(8,128)S(1)} %collective-permute-done.6.rest_3_) | copy-start | bytes 393220
  136.6 22.3 %collective-permute-start.11 = (f32[32,1024]{1,0:T(8,128)}, f32[32,1024]{1,0:T(8,128)S(1)}, u32[]{:S(2)}, u32[]{:S(2)}) collective-permute-start(f32[32,1024]{1,0:T(8,128)} %get-tuple-element.53), channel_id=1, source_target_pairs={{0,16},{2,18},{4,20},{6,22},{8,24},{10,26},{12,28},{14,30},{16,0},... | collective-permute-start | bytes 393224 | tf_op jit(solution)/shard_map/ppermute | solution.py:359
  136.9 46.2 %copy-start.8 = (f32[32,1024]{1,0:T(8,128)}, f32[32,1024]{1,0:T(8,128)S(1)}, u32[]{:S(2)}) copy-start(f32[32,1024]{1,0:T(8,128)S(1)} %collective-permute-done.7.rest_4_) | copy-start | bytes 393220
  136.9 25.0 %collective-permute-start.12 = (f32[32,1024]{1,0:T(8,128)}, f32[32,1024]{1,0:T(8,128)S(1)}, u32[]{:S(2)}, u32[]{:S(2)}) collective-permute-start(f32[32,1024]{1,0:T(8,128)} %get-tuple-element.54), channel_id=1, source_target_pairs={{0,18},{2,16},{4,22},{6,20},{8,26},{10,24},{12,30},{14,28},{16,2},... | collective-permute-start | bytes 393224 | tf_op jit(solution)/shard_map/ppermute | solution.py:359
  139.2 26.8 %collective-permute-start.13 = (f32[32,1024]{1,0:T(8,128)}, f32[32,1024]{1,0:T(8,128)S(1)}, u32[]{:S(2)}, u32[]{:S(2)}) collective-permute-start(f32[32,1024]{1,0:T(8,128)} %get-tuple-element.55), channel_id=1, source_target_pairs={{0,20},{2,22},{4,16},{6,18},{8,28},{10,30},{12,24},{14,26},{16,4},... | collective-permute-start | bytes 393224 | tf_op jit(solution)/shard_map/ppermute | solution.py:359
  145.4 23.5 %collective-permute-start.14 = (f32[32,1024]{1,0:T(8,128)}, f32[32,1024]{1,0:T(8,128)S(1)}, u32[]{:S(2)}, u32[]{:S(2)}) collective-permute-start(f32[32,1024]{1,0:T(8,128)} %get-tuple-element.56), channel_id=1, source_target_pairs={{0,22},{2,20},{4,18},{6,16},{8,30},{10,28},{12,26},{14,24},{16,6},... | collective-permute-start | bytes 393224 | tf_op jit(solution)/shard_map/ppermute | solution.py:359
  148.8 25.7 %collective-permute-start.15 = (f32[32,1024]{1,0:T(8,128)}, f32[32,1024]{1,0:T(8,128)S(1)}, u32[]{:S(2)}, u32[]{:S(2)}) collective-permute-start(f32[32,1024]{1,0:T(8,128)} %get-tuple-element.57), channel_id=1, source_target_pairs={{0,24},{2,26},{4,28},{6,30},{8,16},{10,18},{12,20},{14,22},{16,8},... | collective-permute-start | bytes 393224 | tf_op jit(solution)/shard_map/ppermute | solution.py:359
  158.9 19.9 %collective-permute-start.16 = (f32[32,1024]{1,0:T(8,128)}, f32[32,1024]{1,0:T(8,128)S(1)}, u32[]{:S(2)}, u32[]{:S(2)}) collective-permute-start(f32[32,1024]{1,0:T(8,128)} %get-tuple-element.58), channel_id=1, source_target_pairs={{0,26},{2,24},{4,30},{6,28},{8,18},{10,16},{12,22},{14,20},{16,10}... | collective-permute-start | bytes 393224 | tf_op jit(solution)/shard_map/ppermute | solution.py:359
  161.9 19.2 %collective-permute-start.17 = (f32[32,1024]{1,0:T(8,128)}, f32[32,1024]{1,0:T(8,128)S(1)}, u32[]{:S(2)}, u32[]{:S(2)}) collective-permute-start(f32[32,1024]{1,0:T(8,128)} %get-tuple-element.59), channel_id=1, source_target_pairs={{0,28},{2,30},{4,24},{6,26},{8,20},{10,22},{12,16},{14,18},{16,12}... | collective-permute-start | bytes 393224 | tf_op jit(solution)/shard_map/ppermute | solution.py:359
  166.0 17.1 %collective-permute-start.18 = (f32[32,1024]{1,0:T(8,128)}, f32[32,1024]{1,0:T(8,128)S(1)}, u32[]{:S(2)}, u32[]{:S(2)}) collective-permute-start(f32[32,1024]{1,0:T(8,128)} %get-tuple-element.60), channel_id=1, source_target_pairs={{0,30},{2,28},{4,26},{6,24},{8,22},{10,20},{12,18},{14,16},{16,14}... | collective-permute-start | bytes 393224 | tf_op jit(solution)/shard_map/ppermute | solution.py:359
  (21 other events, 296.2 us)
